TPU v7x, 256 devices: a whole 4x4x8 slice. The times are simulated.
256 devices in a mesh: gx: 16 (over y, x_lo, core), gy: 16 (over x_hi, z).
Axes of the slice: x: 4 (x_hi: 2, x_lo: 2; x = x_hi * 2 + x_lo), y: 4, z: 8, core: 2. Of those that a mesh axis runs over, the one named last changes fastest.
Arguments:
- cotangent: float32 [3, 32, 32, 128], P(None, 'gx', 'gy'), may hold values from -4 to 4
- polarizability: float32 [32, 32, 128], P('gx', 'gy'), may hold values from 0.2 to 1.6
- site_offset: int32 [3, 32, 32, 128], P(None, 'gx', 'gy'), may hold values from 0 to 15, as said below
- site_fraction: float32 [3, 32, 32, 128], P(None, 'gx', 'gy'), may hold values from 0.2 to 0.8
- cell_count: int32 [32, 32, 16], P('gx', 'gy'), may hold values from 4 to 8, as said below
Outputs:
- adjoint_dipoles: float32 [3, 32, 32, 128], P(None, 'gx', 'gy')
Inputs may be any that keep to these rules, and one draw needn't show every extreme that they name: `site_offset`: within a cell the 8 slots name distinct mesh points: no two slots have the same three components. The first component is below 8, the second below 8, the third below 16. `cell_count`: some cell holds 8 live atoms.
All inputs are finite; a program needn't handle non-finite values.
Results may differ from a plain program's by a relative error of at most 0.0001.
Values sent between devices are 32-bit elements; how exact they have to be, the bound alone decides.
A program may use at most 128 MiB of HBM per device.

v0:
```python
import math

import jax
import jax.numpy as jnp
import ml_dtypes
import numpy as np
from jax import lax
from jax.experimental import pallas as pl
from jax.experimental.pallas import tpu as pltpu
from jax.sharding import PartitionSpec as P

BETA = 0.7
THOLE = 0.39
ROOT_PI = 1.7724538509055159
SELF_GAIN = 4.0 * BETA * BETA * BETA / (3.0 * ROOT_PI)
ITERS = 2
N = 256
SIDE = 16
MESH = pl.DeviceIdType.MESH
F32 = jnp.float32
BF16 = jnp.bfloat16

ERFC_P = (
    2.326819970068386e-2,
    -1.387039388740657e-1,
    3.687424674597105e-1,
    -5.824733027278666e-1,
    6.210004621745983e-1,
    -4.944515323274145e-1,
    3.404879937665872e-1,
    -2.741127028184656e-1,
    5.638259427386472e-1,
)
ERFC_R = (
    -1.047766399936249e1,
    1.297719955372516e1,
    -7.495518717768503e0,
    2.921019019210786e0,
    -1.015265279202700e0,
    4.218463358204948e-1,
    -2.820767439740514e-1,
    5.641895067754075e-1,
)
ERF_T = (
    7.853861353153693e-5,
    -8.010193625184903e-4,
    5.188327685732524e-3,
    -2.685381193529856e-2,
    1.128358514861418e-1,
    -3.761262582423300e-1,
    1.128379165726710e0,
)


def halves_np(table):
    high = table.astype(np.float32).astype(ml_dtypes.bfloat16)
    low = (table - high.astype(np.float64)).astype(np.float32).astype(ml_dtypes.bfloat16)
    return high, low


def tables():
    grid = np.arange(N)
    angle = 2.0 * math.pi / N * (grid[:, None] * grid[None, :] % N)
    hartley = np.cos(angle) + np.sin(angle)
    short = np.arange(SIDE)
    pair = (
        short[:, None, None, None] * short[None, None, :, None]
        + short[None, :, None, None] * short[None, None, None, :]
    ).reshape(N, N)
    outer = 2.0 * math.pi / SIDE * (pair % SIDE)
    twist = 2.0 * math.pi / N * (pair % N)

    def part(freq):
        signed = np.where(2 * freq < N, freq, freq - N) / N
        factor = 9.0 / (2.0 + np.cos(2.0 * math.pi * freq / N)) ** 2
        return signed * signed, factor

    low_x = short[:, None, None, None]
    low_y = short[None, :, None, None]
    freq_x = (low_x + SIDE * short[None, None, :, None]) + 0 * low_y
    freq_y = (low_y + SIDE * short[None, None, None, :]) + 0 * low_x
    square_x, factor_x = part(freq_x)
    square_y, factor_y = part(freq_y)
    square = (square_x + square_y).reshape(N, N)
    gain = (
        np.exp(-((math.pi / BETA) ** 2) * (square_x + square_y)) * factor_x * factor_y / math.pi
    ).reshape(N, N) / float(N * N * N)
    return (
        *halves_np(hartley),
        *halves_np(np.cos(outer)),
        *halves_np(-np.sin(outer)),
        np.cos(twist).astype(np.float32),
        (-np.sin(twist)).astype(np.float32),
        gain.astype(np.float32),
        square.astype(np.float32),
    )


TABLES = tables()

NN = (((1,), (0,)), ((), ()))
NT = (((1,), (1,)), ((), ()))


def halves(value):
    high = value.astype(BF16)
    return high, (value - high.astype(F32)).astype(BF16)


def product(left, right, dims=NN):
    def dot(a, b):
        return lax.dot_general(a, b, dims, preferred_element_type=F32)

    return dot(left[0], right[0]) + (dot(left[0], right[1]) + dot(left[1], right[0]))


def polynomial(terms, value):
    total = jnp.full_like(value, terms[0])
    for term in terms[1:]:
        total = total * value + term
    return total


def pair_coefficients(square, root):
    inverse = lax.rsqrt(square)
    distance = square * inverse
    inverse_square = 1.0 / square
    argument = BETA * distance
    steep = argument * argument
    bell = jnp.exp(-steep)
    ratio = inverse * (1.0 / BETA)
    small = ratio * ratio
    tail = jnp.where(
        argument < 2.0, polynomial(ERFC_P, small), polynomial(ERFC_R, small)
    )
    erfc = jnp.where(
        argument < 1.0,
        1.0 - argument * polynomial(ERF_T, steep),
        bell * ratio * tail,
    )
    gauss = (2.0 * BETA / ROOT_PI) * bell
    first = (erfc * inverse + gauss) * inverse_square
    second = (3.0 * first + (2.0 * BETA * BETA) * gauss) * inverse_square
    scaled = THOLE * square * distance * root
    damping = jnp.exp(-scaled)
    inverse_cube = inverse_square * inverse
    first = first - damping * inverse_cube
    second = second - 3.0 * (1.0 + scaled) * damping * inverse_cube * inverse_square
    return first, second


def spline(f):
    rest = 1.0 - f
    square = f * f
    cube = square * f
    values = (
        rest * rest * rest / 6.0,
        (3.0 * cube - 6.0 * square + 4.0) / 6.0,
        (-3.0 * cube + 3.0 * square + 3.0 * f + 1.0) / 6.0,
        cube / 6.0,
    )
    slopes = (
        -0.5 * rest * rest,
        0.5 * (3.0 * square - 4.0 * f),
        0.5 * (-3.0 * square + 2.0 * f + 1.0),
        0.5 * square,
    )
    return values, slopes


def placed(place, weights):
    total = jnp.where(place == 0, weights[0], 0.0)
    for order in range(1, 4):
        total = jnp.where(place == order, weights[order], total)
    return total


def kernel(
    cot, pol, off, frac, cnt, h_hi, h_lo, c_hi, c_lo, s_hi, s_lo, t_re, t_im, gain, square_xy,
    out,
    fixed, moving, own, prod, wz_hi, wz_lo, p_hi, p_lo, spread, send_a, send_b, land_a, land_b,
    near_static, near_moving, tensor, near, far, far_in,
    send_s, recv_s, halo_send, halo_recv, part_send, part_recv, second_level,
):
    mx = lax.axis_index("gx")
    my = lax.axis_index("gy")
    me = mx * SIDE + my

    def wrap(i):
        return lax.rem(i + SIDE, SIDE)

    entry = pltpu.get_barrier_semaphore()

    def greet(i, carry):
        pl.semaphore_signal(entry, inc=1, device_id=(wrap(mx + i), my), device_id_type=MESH)
        pl.semaphore_signal(entry, inc=1, device_id=(mx, wrap(my + i)), device_id_type=MESH)
        return carry

    lax.fori_loop(1, SIDE, greet, 0)
    for a in (-1, 1):
        for b in (-1, 1):
            pl.semaphore_signal(
                entry, inc=1, device_id=(wrap(mx + a), wrap(my + b)), device_id_type=MESH
            )

    lane = lax.broadcasted_iota(jnp.int32, (8, 128), 1)
    row = lax.broadcasted_iota(jnp.int32, (8, 128), 0)
    expand = (
        lax.broadcasted_iota(jnp.int32, (16, 128), 1) // 8
        == lax.broadcasted_iota(jnp.int32, (16, 128), 0)
    ).astype(F32)
    slot = (lax.broadcasted_iota(jnp.int32, (2, 128), 1) % 8).astype(F32)
    for cx in range(2):
        counts = jnp.dot(cnt[cx].astype(F32), expand, preferred_element_type=F32)
        weight = jnp.where(slot < counts, 1.0, 0.0) * pol[cx]
        for cy in range(2):
            w = weight[cy : cy + 1]
            c3 = [cot[c, cx, cy : cy + 1] for c in range(3)]
            zero = jnp.zeros((1, 128), F32)
            fixed[cx + 1, cy + 1] = jnp.concatenate(
                [off[c, cx, cy : cy + 1].astype(F32) for c in range(3)]
                + [frac[c, cx, cy : cy + 1] for c in range(3)]
                + [pol[cx, cy : cy + 1], zero],
                axis=0,
            )
            own[cx, cy] = jnp.concatenate(c3 + [w, zero, zero, zero, zero], axis=0)
            moving[0, cx + 1, cy + 1] = jnp.concatenate(
                [w * c3[c] for c in range(3)] + [zero] * 5, axis=0
            )

    pl.semaphore_wait(entry, 2 * (SIDE - 1) + 4)

    def second(i, carry):
        pl.semaphore_signal(
            second_level, inc=1, device_id=(wrap(mx + i), my), device_id_type=MESH
        )
        return carry

    lax.fori_loop(1, SIDE, second, 0)

    def halo(ref, slot_of):
        copies = []
        k = 0
        for a in (-1, 0, 1):
            for b in (-1, 0, 1):
                if a == 0 and b == 0:
                    continue
                src_x = {-1: pl.ds(1, 1), 0: pl.ds(1, 2), 1: pl.ds(2, 1)}[a]
                src_y = {-1: pl.ds(1, 1), 0: pl.ds(1, 2), 1: pl.ds(2, 1)}[b]
                dst_x = {-1: pl.ds(3, 1), 0: pl.ds(1, 2), 1: pl.ds(0, 1)}[a]
                dst_y = {-1: pl.ds(3, 1), 0: pl.ds(1, 2), 1: pl.ds(0, 1)}[b]
                copies.append(
                    pltpu.make_async_remote_copy(
                        src_ref=ref.at[src_x, src_y],
                        dst_ref=ref.at[dst_x, dst_y],
                        send_sem=halo_send.at[slot_of, k],
                        recv_sem=halo_recv.at[slot_of, k],
                        device_id=(wrap(mx + a), wrap(my + b)),
                        device_id_type=MESH,
                    )
                )
                k += 1
        return copies

    first_halo = halo(fixed, 2) + halo(moving.at[0], 0)
    for copy in first_halo:
        copy.start()
    for copy in first_halo:
        copy.wait()

    pick = [((lane // 8 + dz + 16) % 16) * 8 + row for dz in (-1, 0, 1)]

    def expanded(line, k):
        return jnp.take_along_axis(
            jnp.broadcast_to(line, (8, 128)), pick[k], axis=1, mode="promise_in_bounds"
        )

    def grow_static(col, carry):
        tile = fixed[col // 4, lax.rem(col, 4)]
        lines = [tile[c : c + 1] + 1.0 + tile[c + 3 : c + 4] for c in range(3)] + [tile[6:7]]
        for k in range(3):
            for c in range(4):
                value = expanded(lines[c], k)
                if c == 2:
                    value = value + 16.0 * (k - 1)
                near_static[col, k, c] = value
        return carry

    def grow_moving(it):
        def body(col, carry):
            tile = moving[it, col // 4, lax.rem(col, 4)]
            for k in range(3):
                for c in range(3):
                    near_moving[col, k, c] = expanded(tile[c : c + 1], k)
            return carry

        lax.fori_loop(0, 16, body, 0)

    tall = lax.broadcasted_iota(jnp.int32, (N, 128), 0)
    low = lax.broadcasted_iota(jnp.int32, (SIDE, 128), 0)
    cell_z = lax.broadcasted_iota(jnp.int32, (1, 128), 1) // 8 * 16

    def weights(col, carry):
        ex = col // 3
        ey = lax.rem(col, 3)
        tile = fixed[ex, ey]
        anchor = tile[0:3].astype(jnp.int32)
        value, slope = zip(*[spline(tile[c + 3 : c + 4]) for c in range(3)])
        place_x = low - (anchor[0:1] + (ex - 1) * 8)
        place_y = low - (anchor[1:2] + (ey - 1) * 8)
        place_z = (tall - (anchor[2:3] + cell_z)) & (N - 1)
        wx, sx = placed(place_x, value[0]), placed(place_x, slope[0])
        wy, sy = placed(place_y, value[1]), placed(place_y, slope[1])
        for x in range(SIDE):
            rows = pl.ds(x * SIDE, SIDE)
            prod[col, 0, rows] = sx[x : x + 1] * wy
            prod[col, 1, rows] = wx[x : x + 1] * sy
            prod[col, 2, rows] = wx[x : x + 1] * wy
        for k, source in enumerate((value[2], slope[2])):
            high, rest = halves(placed(place_z, source))
            wz_hi[col, :, pl.ds(128 * k, 128)] = high
            wz_lo[col, :, pl.ds(128 * k, 128)] = rest
        return carry

    lax.fori_loop(0, 9, weights, 0)

    def pairs(item, carry):
        q = item // 9
        nb = lax.rem(item, 9)
        cx = q // 2
        cy = lax.rem(q, 2)
        dx = nb // 3 - 1
        dy = lax.rem(nb, 3) - 1
        tile = fixed[cx + 1, cy + 1]
        here = [tile[c : c + 1] + 1.0 + tile[c + 3 : c + 4] for c in range(3)]
        here[0] = here[0] - (8 * dx).astype(F32)
        here[1] = here[1] - (8 * dy).astype(F32)
        mine = tile[6:7]
        col = (cx + 1 + dx) * 4 + cy + 1 + dy
        for k in range(3):
            apart = [here[c] - near_static[col, k, c] for c in range(3)]
            square = apart[0] * apart[0] + apart[1] * apart[1] + apart[2] * apart[2]
            root = lax.rsqrt(mine * near_static[col, k, 3])
            if k == 1:
                same = (row == lane % 8) & (nb == 4)
                square = jnp.where(same, 1.0, square)
            c1, c2 = pair_coefficients(square, root)
            if k == 1:
                c1 = jnp.where(same, 0.0, c1)
                c2 = jnp.where(same, 0.0, c2)
            scaled = [c2 * apart[c] for c in range(3)]
            tensor[item, k, 0] = scaled[0] * apart[0] - c1
            tensor[item, k, 1] = scaled[1] * apart[1] - c1
            tensor[item, k, 2] = scaled[2] * apart[2] - c1
            tensor[item, k, 3] = scaled[0] * apart[1]
            tensor[item, k, 4] = scaled[0] * apart[2]
            tensor[item, k, 5] = scaled[1] * apart[2]
        return carry

    def near_field(it):
        grow_moving(it)

        def body(q, carry):
            cx = q // 2
            cy = lax.rem(q, 2)

            def inner(nb, total):
                fx, fy, fz = total
                col = (cx + nb // 3) * 4 + cy + lax.rem(nb, 3)
                item = q * 9 + nb
                for k in range(3):
                    vx, vy, vz = [near_moving[col, k, c] for c in range(3)]
                    xx, yy, zz, xy, xz, yz = [tensor[item, k, c] for c in range(6)]
                    fx = fx + (xx * vx + xy * vy + xz * vz)
                    fy = fy + (xy * vx + yy * vy + yz * vz)
                    fz = fz + (xz * vx + yz * vy + zz * vz)
                return fx, fy, fz

            zero = jnp.zeros((8, 128), F32)
            sums = lax.fori_loop(0, 9, inner, (zero, zero, zero))
            near[q] = jnp.concatenate(
                [jnp.sum(s, axis=0, keepdims=True) for s in sums]
                + [jnp.zeros((5, 128), F32)],
                axis=0,
            )
            return carry

        lax.fori_loop(0, 4, body, 0)

    def exchange(source, target, k):
        def copy(t):
            return pltpu.make_async_remote_copy(
                src_ref=source.at[t],
                dst_ref=target.at[me],
                send_sem=send_s.at[k],
                recv_sem=recv_s.at[k],
                device_id=(t // SIDE, lax.rem(t, SIDE)),
                device_id_type=MESH,
            )

        def send(i, carry):
            copy(lax.rem(me + i, N)).start()
            return carry

        lax.fori_loop(1, N, send, 0)
        target[me] = source[me]

    def arrive(source, target, k):
        pltpu.make_async_remote_copy(
            src_ref=source.at[pl.ds(0, N - 1)],
            dst_ref=target.at[pl.ds(0, N - 1)],
            send_sem=send_s.at[k],
            recv_sem=recv_s.at[k],
            device_id=(mx, wrap(my + 1)),
            device_id_type=MESH,
        ).wait()

    hartley = (h_hi, h_lo)

    def loaded(pair):
        return pair[0][...], pair[1][...]

    def put_rows(ref, value):
        ref[:, 0, :] = value[:, :128]
        ref[:, 1, :] = value[:, 128:]

    def get_rows(ref):
        return jnp.concatenate([ref[:, 0, :], ref[:, 1, :]], axis=1)

    def filtered(value):
        cosine = (c_hi[...], c_lo[...])
        sine = (s_hi[...], s_lo[...])
        parts = halves(value)
        re = product(cosine, parts)
        im = product(sine, parts)
        tr, ti = t_re[...], t_im[...]
        first = halves(re * tr - im * ti)
        other = halves(re * ti + im * tr)
        re = product(first, cosine) - product(other, sine)
        im = product(first, sine) + product(other, cosine)
        line = jnp.zeros((1, 128), F32) + me.astype(F32)
        signed = jnp.where(line < N // 2, line, line - N) * (1.0 / N)
        height = signed * signed
        bend = 2.0 + jnp.cos(line * (2.0 * math.pi / N))
        strength = jnp.exp(-((math.pi / BETA) ** 2) * height) * 9.0 / (bend * bend)
        height = jnp.concatenate([height, height], axis=1)
        strength = jnp.concatenate([strength, strength], axis=1)
        square = square_xy[...] + height
        centre = square == 0.0
        green = jnp.where(
            centre, 0.0, gain[...] * strength / jnp.where(centre, 1.0, square)
        )
        first = halves(re * green)
        other = halves(im * green)
        re = product(first, cosine) + product(other, sine)
        im = product(other, cosine) - product(first, sine)
        first = halves(re * tr + im * ti)
        other = halves(im * tr - re * ti)
        return product(cosine, first) + product(sine, other)

    def iteration(it, carry):
        def rows(col, carry):
            tile = moving[it, col // 3, lax.rem(col, 3)]
            plain = tile[0:1] * prod[col, 0] + tile[1:2] * prod[col, 1]
            steep = tile[2:3] * prod[col, 2]
            lanes = pl.ds(pl.multiple_of(col * N, N), 128)
            lanes_2 = pl.ds(pl.multiple_of(col * N + 128, 128), 128)
            p_hi[:, lanes], p_lo[:, lanes] = halves(plain)
            p_hi[:, lanes_2], p_lo[:, lanes_2] = halves(steep)
            return carry

        lax.fori_loop(0, 9, rows, 0)
        spread[...] = jnp.zeros((N, N), F32)

        def accumulate(col, carry):
            lanes = pl.ds(pl.multiple_of(col * N, N), N)
            spread[...] += product(
                (wz_hi[col], wz_lo[col]), (p_hi[:, lanes], p_lo[:, lanes]), NT
            )
            return carry

        lax.fori_loop(0, 9, accumulate, 0)
        put_rows(send_a, product(loaded(hartley), halves(spread[...])))

        @pl.when(it == 0)
        def _():
            pl.semaphore_wait(second_level, SIDE - 1)

        exchange(send_a, land_a.at[it], 2 * it)

        @pl.when(it == 0)
        def _():
            lax.fori_loop(0, 16, grow_static, 0)
            lax.fori_loop(0, 36, pairs, 0)

        arrive(send_a, land_a.at[it], 2 * it)
        put_rows(send_b, filtered(get_rows(land_a.at[it])))
        exchange(send_b, land_b.at[it], 2 * it + 1)
        near_field(it)
        arrive(send_b, land_b.at[it], 2 * it + 1)
        potential = product(loaded(hartley), halves(get_rows(land_b.at[it])))
        spread[...] = potential.T

        def gather(col, carry):
            sampled = product(halves(spread[...]), (wz_hi[col], wz_lo[col]))
            plain = sampled[:, :128]
            steep = sampled[:, 128:]
            far[col // 3, lax.rem(col, 3)] = jnp.concatenate(
                [
                    jnp.sum(prod[col, 0] * plain, axis=0, keepdims=True),
                    jnp.sum(prod[col, 1] * plain, axis=0, keepdims=True),
                    jnp.sum(prod[col, 2] * steep, axis=0, keepdims=True),
                    jnp.zeros((5, 128), F32),
                ],
                axis=0,
            )
            return carry

        lax.fori_loop(0, 9, gather, 0)
        copies = []
        for k, (a, b) in enumerate(((1, 0), (0, 1), (1, 1))):
            span_x = pl.ds(0, 1) if a else pl.ds(1, 2)
            span_y = pl.ds(0, 1) if b else pl.ds(1, 2)
            land_x = pl.ds(0, 1) if a else pl.ds(0, 2)
            land_y = pl.ds(0, 1) if b else pl.ds(0, 2)
            copies.append(
                pltpu.make_async_remote_copy(
                    src_ref=far.at[span_x, span_y],
                    dst_ref=far_in.at[it, k, land_x, land_y],
                    send_sem=part_send.at[it, k],
                    recv_sem=part_recv.at[it, k],
                    device_id=(wrap(mx - a), wrap(my - b)),
                    device_id_type=MESH,
                )
            )
        for copy in copies:
            copy.start()
        for copy in copies:
            copy.wait()
        for cx in range(2):
            for cy in range(2):
                total = far[cx + 1, cy + 1]
                if cx == 1:
                    total = total + far_in[it, 0, 0, cy]
                if cy == 1:
                    total = total + far_in[it, 1, cx, 0]
                if cx == 1 and cy == 1:
                    total = total + far_in[it, 2, 0, 0]
                field = (
                    near[2 * cx + cy] - total + SELF_GAIN * moving[it, cx + 1, cy + 1]
                )
                tile = own[cx, cy]
                result = tile[3:4] * (tile + field)
                moving[it + 1, cx + 1, cy + 1] = result
                for c in range(3):
                    out[c, cx, cy : cy + 1] = result[c : c + 1]

        @pl.when(it == 0)
        def _():
            copies = halo(moving.at[1], 1)
            for copy in copies:
                copy.start()
            for copy in copies:
                copy.wait()

        return carry

    lax.fori_loop(0, ITERS, iteration, 0)


def shards(cotangent, polarizability, site_offset, site_fraction, cell_count):
    vmem = pl.BlockSpec(memory_space=pltpu.VMEM)

    def room(*shape, dtype=F32):
        return pltpu.VMEM(shape, dtype)

    dma = pltpu.SemaphoreType.DMA
    return pl.pallas_call(
        kernel,
        out_shape=jax.ShapeDtypeStruct((3, 2, 2, 128), F32),
        in_specs=[vmem] * (5 + len(TABLES)),
        out_specs=vmem,
        scratch_shapes=[
            room(4, 4, 8, 128),
            room(3, 4, 4, 8, 128),
            room(2, 2, 8, 128),
            room(9, 3, N, 128),
            room(9, N, N, dtype=BF16),
            room(9, N, N, dtype=BF16),
            room(N, 9 * N, dtype=BF16),
            room(N, 9 * N, dtype=BF16),
            room(N, N),
            room(N, 2, 128),
            room(N, 2, 128),
            room(2, N, 2, 128),
            room(2, N, 2, 128),
            room(16, 3, 4, 8, 128),
            room(16, 3, 3, 8, 128),
            room(36, 3, 6, 8, 128),
            room(4, 8, 128),
            room(3, 3, 8, 128),
            room(2, 3, 2, 2, 8, 128),
            dma((4,)),
            dma((4,)),
            dma((3, 8)),
            dma((3, 8)),
            dma((2, 3)),
            dma((2, 3)),
            pltpu.SemaphoreType.REGULAR,
        ],
        compiler_params=pltpu.CompilerParams(
            collective_id=0, has_side_effects=True, vmem_limit_bytes=56 * 1024 * 1024
        ),
    )(
        cotangent,
        polarizability,
        site_offset,
        site_fraction,
        cell_count,
        *[jnp.asarray(table) for table in TABLES],
    )


def solution(mesh):
    return jax.shard_map(
        shards,
        mesh=mesh,
        in_specs=(
            P(None, "gx", "gy", None),
            P("gx", "gy", None),
            P(None, "gx", "gy", None),
            P(None, "gx", "gy", None),
            P("gx", "gy", None),
        ),
        out_specs=P(None, "gx", "gy", None),
        check_vma=False,
    )
```

profile of v0, /device:TPU:1, one launch (start us, length us, event | category | flops | bytes accessed | tf_op | source)
XLA Modules:
  0.0 95.1 jit_solution(5476886770023261497)
XLA Ops:
  0.0 93.8 %shard_map.145 = f32[3,2,2,128]{3,2,1,0:T(2,128)} custom-call(f32[3,2,2,128]{3,2,1,0:T(2,128)} %cot.1, f32[2,2,128]{2,1,0:T(2,128)} %pol.1, s32[3,2,2,128]{3,2,1,0:T(2,128)} %off.1, f32[3,2,2,128]{3,2,1,0:T(2,128)} %frac.1, s32[2,2,16]{2,1,0:T(2,128)} %cnt.1, bf16[256,256]{1,0:T(8,128)(2,1)} %constant.20.clone.h_hi, bf16[256,256]{1,0:T(8,128)(2,1)} %constant.21.clone.h_lo, ...), custom_call_target="tpu_custom_call" | custom-call | tf_op jit(solution)/shard_map/pallas_call | solution.py:578
  93.8 1.3 %copy.17 = f32[3,2,2,128]{3,2,1,0:T(2,128)} copy(f32[3,2,2,128]{3,2,1,0:T(2,128)} %shard_map.145) | data formatting | bytes 12288
where the time goes:
time: 95.2 us; the launch traced here: 95.1 us
  Pallas kernels  93.8 us (99%)
  local copies, waits for them, and re-layouts  1.29 us (1%)
    pallas_call x1, Pallas kernels, shards(): pl.pallas_call(kernel, out_shape=jax.ShapeDtypeStruct((3, 2, 2, 128), F32...  93.8 us

commit v1 on v0

--- a/solution.py
+++ b/solution.py
@@ -16,6 +16,7 @@
 ITERS = 2
 N = 256
 SIDE = 16
+HALF = SIDE * (SIDE // 2 + 1)
 MESH = pl.DeviceIdType.MESH
 F32 = jnp.float32
 BF16 = jnp.bfloat16
@@ -85,15 +86,11 @@
     gain = (
         np.exp(-((math.pi / BETA) ** 2) * (square_x + square_y)) * factor_x * factor_y / math.pi
     ).reshape(N, N) / float(N * N * N)
-    return (
-        *halves_np(hartley),
-        *halves_np(np.cos(outer)),
-        *halves_np(-np.sin(outer)),
-        np.cos(twist).astype(np.float32),
-        (-np.sin(twist)).astype(np.float32),
-        gain.astype(np.float32),
-        square.astype(np.float32),
-    )
+    twice = np.where((grid // SIDE == 0) | (grid // SIDE == SIDE // 2), 1.0, 2.0)
+    gain = gain * twice[:, None]
+    waves = np.stack(halves_np(np.concatenate([hartley, np.cos(outer), -np.sin(outer)], axis=0)))
+    plane = np.stack([np.cos(twist), -np.sin(twist), gain, square])[:, :HALF].astype(np.float32)
+    return waves, plane
 
 
 TABLES = tables()
@@ -111,7 +108,9 @@
     def dot(a, b):
         return lax.dot_general(a, b, dims, preferred_element_type=F32)
 
-    return dot(left[0], right[0]) + (dot(left[0], right[1]) + dot(left[1], right[0]))
+    count = left[0].shape[0]
+    both = dot(jnp.concatenate(left, axis=0), right[0])
+    return both[:count] + (both[count:] + dot(left[0], right[1]))
 
 
 def polynomial(terms, value):
@@ -176,11 +175,11 @@
 
 
 def kernel(
-    cot, pol, off, frac, cnt, h_hi, h_lo, c_hi, c_lo, s_hi, s_lo, t_re, t_im, gain, square_xy,
+    cot, pol, off, frac, cnt, waves_far, plane_far,
     out,
-    fixed, moving, own, prod, wz_hi, wz_lo, p_hi, p_lo, spread, send_a, send_b, land_a, land_b,
-    near_static, near_moving, tensor, near, far, far_in,
-    send_s, recv_s, halo_send, halo_recv, part_send, part_recv, second_level,
+    waves, plane, fixed, moving, prod, wz_hi, wz_lo, wt_hi, wt_lo, p_hi, p_lo, spread,
+    send_a, send_b, land_a, land_b, near_static, near_moving, tensor, near, part, inbox, last_in,
+    table_sem, send_s, recv_s, halo_send, halo_recv, part_send, part_recv, second_level,
 ):
     mx = lax.axis_index("gx")
     my = lax.axis_index("gy")
@@ -202,6 +201,13 @@
             pl.semaphore_signal(
                 entry, inc=1, device_id=(wrap(mx + a), wrap(my + b)), device_id_type=MESH
             )
+
+    table_copies = [
+        pltpu.make_async_copy(waves_far, waves, table_sem.at[0]),
+        pltpu.make_async_copy(plane_far, plane, table_sem.at[1]),
+    ]
+    for copy in table_copies:
+        copy.start()
 
     lane = lax.broadcasted_iota(jnp.int32, (8, 128), 1)
     row = lax.broadcasted_iota(jnp.int32, (8, 128), 0)
@@ -214,18 +220,14 @@
         counts = jnp.dot(cnt[cx].astype(F32), expand, preferred_element_type=F32)
         weight = jnp.where(slot < counts, 1.0, 0.0) * pol[cx]
         for cy in range(2):
-            w = weight[cy : cy + 1]
-            c3 = [cot[c, cx, cy : cy + 1] for c in range(3)]
-            zero = jnp.zeros((1, 128), F32)
+            here = slice(cy, cy + 1)
             fixed[cx + 1, cy + 1] = jnp.concatenate(
-                [off[c, cx, cy : cy + 1].astype(F32) for c in range(3)]
-                + [frac[c, cx, cy : cy + 1] for c in range(3)]
-                + [pol[cx, cy : cy + 1], zero],
+                [off[c, cx, here].astype(F32) for c in range(3)]
+                + [frac[c, cx, here] for c in range(3)]
+                + [pol[cx, here], weight[here]]
+                + [cot[c, cx, here] for c in range(3)]
+                + [jnp.zeros((5, 128), F32)],
                 axis=0,
-            )
-            own[cx, cy] = jnp.concatenate(c3 + [w, zero, zero, zero, zero], axis=0)
-            moving[0, cx + 1, cy + 1] = jnp.concatenate(
-                [w * c3[c] for c in range(3)] + [zero] * 5, axis=0
             )
 
     pl.semaphore_wait(entry, 2 * (SIDE - 1) + 4)
@@ -236,37 +238,45 @@
         )
         return carry
 
-    lax.fori_loop(1, SIDE, second, 0)
-
-    def halo(ref, slot_of):
-        copies = []
-        k = 0
-        for a in (-1, 0, 1):
-            for b in (-1, 0, 1):
-                if a == 0 and b == 0:
-                    continue
-                src_x = {-1: pl.ds(1, 1), 0: pl.ds(1, 2), 1: pl.ds(2, 1)}[a]
-                src_y = {-1: pl.ds(1, 1), 0: pl.ds(1, 2), 1: pl.ds(2, 1)}[b]
-                dst_x = {-1: pl.ds(3, 1), 0: pl.ds(1, 2), 1: pl.ds(0, 1)}[a]
-                dst_y = {-1: pl.ds(3, 1), 0: pl.ds(1, 2), 1: pl.ds(0, 1)}[b]
-                copies.append(
-                    pltpu.make_async_remote_copy(
-                        src_ref=ref.at[src_x, src_y],
-                        dst_ref=ref.at[dst_x, dst_y],
-                        send_sem=halo_send.at[slot_of, k],
-                        recv_sem=halo_recv.at[slot_of, k],
-                        device_id=(wrap(mx + a), wrap(my + b)),
-                        device_id_type=MESH,
-                    )
-                )
-                k += 1
-        return copies
-
-    first_halo = halo(fixed, 2) + halo(moving.at[0], 0)
+    sides = [(a, b) for a in (-1, 0, 1) for b in (-1, 0, 1) if (a, b) != (0, 0)]
+
+    def spans(table, a, b):
+        return tuple(pl.ds(*table[side]) for side in (a, b))
+
+    first_halo = []
+    for k, (a, b) in enumerate(sides):
+        first_halo.append(
+            pltpu.make_async_remote_copy(
+                src_ref=fixed.at[spans({-1: (1, 1), 0: (1, 2), 1: (2, 1)}, a, b)],
+                dst_ref=fixed.at[spans({-1: (3, 1), 0: (1, 2), 1: (0, 1)}, a, b)],
+                send_sem=halo_send.at[0, k],
+                recv_sem=halo_recv.at[0, k],
+                device_id=(wrap(mx + a), wrap(my + b)),
+                device_id_type=MESH,
+            )
+        )
     for copy in first_halo:
         copy.start()
-    for copy in first_halo:
-        copy.wait()
+    lax.fori_loop(1, SIDE, second, 0)
+
+    taken = {-1: (2, 1), 0: (0, 3), 1: (0, 2)}
+    inner = {-1: (0, 1), 0: (0, 3), 1: (0, 2)}
+
+    def part_copies():
+        copies = []
+        for a, b in sides:
+            k = sides.index((-a, -b))
+            copies.append(
+                pltpu.make_async_remote_copy(
+                    src_ref=part.at[spans(taken, -a, -b)],
+                    dst_ref=inbox.at[(k, *spans(inner, -a, -b))],
+                    send_sem=halo_send.at[1, k],
+                    recv_sem=halo_recv.at[1, k],
+                    device_id=(wrap(mx + a), wrap(my + b)),
+                    device_id_type=MESH,
+                )
+            )
+        return copies
 
     pick = [((lane // 8 + dz + 16) % 16) * 8 + row for dz in (-1, 0, 1)]
 
@@ -300,7 +310,7 @@
     low = lax.broadcasted_iota(jnp.int32, (SIDE, 128), 0)
     cell_z = lax.broadcasted_iota(jnp.int32, (1, 128), 1) // 8 * 16
 
-    def weights(col, carry):
+    def weights(col):
         ex = col // 3
         ey = lax.rem(col, 3)
         tile = fixed[ex, ey]
@@ -317,12 +327,30 @@
             prod[col, 1, rows] = wx[x : x + 1] * sy
             prod[col, 2, rows] = wx[x : x + 1] * wy
         for k, source in enumerate((value[2], slope[2])):
-            high, rest = halves(placed(place_z, source))
-            wz_hi[col, :, pl.ds(128 * k, 128)] = high
-            wz_lo[col, :, pl.ds(128 * k, 128)] = rest
-        return carry
-
-    lax.fori_loop(0, 9, weights, 0)
+            full = placed(place_z, source)
+            lanes = pl.ds(pl.multiple_of(col * N + 128 * k, 128), 128)
+            wz_hi[:, lanes], wz_lo[:, lanes] = halves(full)
+            wt_hi[lanes, :], wt_lo[lanes, :] = halves(full.T)
+
+    def weights_own(i, carry):
+        weights((1 + i // 2) * 3 + 1 + lax.rem(i, 2))
+        return carry
+
+    def weights_other(i, carry):
+        weights(i + 2 * (i // 4))
+        return carry
+
+    lax.fori_loop(0, 4, weights_own, 0)
+    for copy in first_halo:
+        copy.wait()
+    lax.fori_loop(0, 5, weights_other, 0)
+
+    def first_moment(col, carry):
+        tile = fixed[col // 4, lax.rem(col, 4)]
+        moving[0, col // 4, lax.rem(col, 4)] = tile[7:8] * tile[8:16]
+        return carry
+
+    lax.fori_loop(0, 16, first_moment, 0)
 
     def pairs(item, carry):
         q = item // 9
@@ -415,10 +443,8 @@
             device_id_type=MESH,
         ).wait()
 
-    hartley = (h_hi, h_lo)
-
-    def loaded(pair):
-        return pair[0][...], pair[1][...]
+    def wave(k):
+        return waves[0, N * k : N * (k + 1)], waves[1, N * k : N * (k + 1)]
 
     def put_rows(ref, value):
         ref[:, 0, :] = value[:, :128]
@@ -428,16 +454,19 @@
         return jnp.concatenate([ref[:, 0, :], ref[:, 1, :]], axis=1)
 
     def filtered(value):
-        cosine = (c_hi[...], c_lo[...])
-        sine = (s_hi[...], s_lo[...])
-        parts = halves(value)
-        re = product(cosine, parts)
-        im = product(sine, parts)
-        tr, ti = t_re[...], t_im[...]
-        first = halves(re * tr - im * ti)
-        other = halves(re * ti + im * tr)
-        re = product(first, cosine) - product(other, sine)
-        im = product(first, sine) + product(other, cosine)
+        cosine = wave(1)
+        sine = wave(2)
+        upper = tuple(
+            jnp.concatenate([c[:HALF], s[:HALF]], axis=0) for c, s in zip(cosine, sine)
+        )
+        both = product(upper, halves(value))
+        re, im = both[:HALF], both[HALF:]
+        tr, ti = plane[0], plane[1]
+        both = halves(jnp.concatenate([re * tr - im * ti, re * ti + im * tr], axis=0))
+        by_cosine = product(both, cosine)
+        by_sine = product(both, sine)
+        re = by_cosine[:HALF] - by_sine[HALF:]
+        im = by_sine[:HALF] + by_cosine[HALF:]
         line = jnp.zeros((1, 128), F32) + me.astype(F32)
         signed = jnp.where(line < N // 2, line, line - N) * (1.0 / N)
         height = signed * signed
@@ -445,42 +474,45 @@
         strength = jnp.exp(-((math.pi / BETA) ** 2) * height) * 9.0 / (bend * bend)
         height = jnp.concatenate([height, height], axis=1)
         strength = jnp.concatenate([strength, strength], axis=1)
-        square = square_xy[...] + height
+        square = plane[3] + height
         centre = square == 0.0
         green = jnp.where(
-            centre, 0.0, gain[...] * strength / jnp.where(centre, 1.0, square)
+            centre, 0.0, plane[2] * strength / jnp.where(centre, 1.0, square)
         )
-        first = halves(re * green)
-        other = halves(im * green)
-        re = product(first, cosine) + product(other, sine)
-        im = product(other, cosine) - product(first, sine)
+        both = halves(jnp.concatenate([re * green, im * green], axis=0))
+        by_cosine = product(both, cosine)
+        by_sine = product(both, sine)
+        re = by_cosine[:HALF] + by_sine[HALF:]
+        im = by_cosine[HALF:] - by_sine[:HALF]
         first = halves(re * tr + im * ti)
         other = halves(im * tr - re * ti)
+        cosine = tuple(c[:, :HALF] for c in cosine)
+        sine = tuple(c[:, :HALF] for c in sine)
         return product(cosine, first) + product(sine, other)
 
     def iteration(it, carry):
-        def rows(col, carry):
-            tile = moving[it, col // 3, lax.rem(col, 3)]
-            plain = tile[0:1] * prod[col, 0] + tile[1:2] * prod[col, 1]
-            steep = tile[2:3] * prod[col, 2]
-            lanes = pl.ds(pl.multiple_of(col * N, N), 128)
-            lanes_2 = pl.ds(pl.multiple_of(col * N + 128, 128), 128)
-            p_hi[:, lanes], p_lo[:, lanes] = halves(plain)
-            p_hi[:, lanes_2], p_lo[:, lanes_2] = halves(steep)
-            return carry
-
-        lax.fori_loop(0, 9, rows, 0)
-        spread[...] = jnp.zeros((N, N), F32)
-
-        def accumulate(col, carry):
-            lanes = pl.ds(pl.multiple_of(col * N, N), N)
-            spread[...] += product(
-                (wz_hi[col], wz_lo[col]), (p_hi[:, lanes], p_lo[:, lanes]), NT
-            )
-            return carry
-
-        lax.fori_loop(0, 9, accumulate, 0)
-        put_rows(send_a, product(loaded(hartley), halves(spread[...])))
+        for group in range(3):
+            for col in range(3 * group, 3 * group + 3):
+                tile = moving[it, col // 3, col % 3]
+                plain = tile[0:1] * prod[col, 0] + tile[1:2] * prod[col, 1]
+                steep = tile[2:3] * prod[col, 2]
+                left = slice(col * N, col * N + 128)
+                right = slice(col * N + 128, col * N + N)
+                p_hi[:, left], p_lo[:, left] = halves(plain)
+                p_hi[:, right], p_lo[:, right] = halves(steep)
+            span = slice(3 * N * group, 3 * N * (group + 1))
+            term = product((p_hi[:, span], p_lo[:, span]), (wt_hi[span], wt_lo[span]))
+            if group == 0:
+                spread[...] = term
+            else:
+                spread[...] += term
+
+        @pl.when(it == 0)
+        def _():
+            for copy in table_copies:
+                copy.wait()
+
+        put_rows(send_a, product(wave(0), halves(spread[...]), NT))
 
         @pl.when(it == 0)
         def _():
@@ -498,70 +530,92 @@
         exchange(send_b, land_b.at[it], 2 * it + 1)
         near_field(it)
         arrive(send_b, land_b.at[it], 2 * it + 1)
-        potential = product(loaded(hartley), halves(get_rows(land_b.at[it])))
-        spread[...] = potential.T
-
-        def gather(col, carry):
-            sampled = product(halves(spread[...]), (wz_hi[col], wz_lo[col]))
+        potential = product(wave(0), halves(get_rows(land_b.at[it])))
+        turned = halves(potential.T)
+
+        def gather(col):
+            lanes = slice(col * N, col * N + N)
+            sampled = product(turned, (wz_hi[:, lanes], wz_lo[:, lanes]))
             plain = sampled[:, :128]
             steep = sampled[:, 128:]
-            far[col // 3, lax.rem(col, 3)] = jnp.concatenate(
+            ex, ey = col // 3, col % 3
+            total = jnp.concatenate(
                 [
-                    jnp.sum(prod[col, 0] * plain, axis=0, keepdims=True),
-                    jnp.sum(prod[col, 1] * plain, axis=0, keepdims=True),
-                    jnp.sum(prod[col, 2] * steep, axis=0, keepdims=True),
+                    -jnp.sum(prod[col, 0] * plain, axis=0, keepdims=True),
+                    -jnp.sum(prod[col, 1] * plain, axis=0, keepdims=True),
+                    -jnp.sum(prod[col, 2] * steep, axis=0, keepdims=True),
                     jnp.zeros((5, 128), F32),
                 ],
                 axis=0,
             )
-            return carry
-
-        lax.fori_loop(0, 9, gather, 0)
-        copies = []
-        for k, (a, b) in enumerate(((1, 0), (0, 1), (1, 1))):
-            span_x = pl.ds(0, 1) if a else pl.ds(1, 2)
-            span_y = pl.ds(0, 1) if b else pl.ds(1, 2)
-            land_x = pl.ds(0, 1) if a else pl.ds(0, 2)
-            land_y = pl.ds(0, 1) if b else pl.ds(0, 2)
-            copies.append(
-                pltpu.make_async_remote_copy(
-                    src_ref=far.at[span_x, span_y],
-                    dst_ref=far_in.at[it, k, land_x, land_y],
-                    send_sem=part_send.at[it, k],
-                    recv_sem=part_recv.at[it, k],
-                    device_id=(wrap(mx - a), wrap(my - b)),
-                    device_id_type=MESH,
+            if ex >= 1 and ey >= 1:
+                total = total + near[2 * ex + ey - 3] + SELF_GAIN * moving[it, ex, ey]
+            part[ex, ey] = total
+
+        for col in (0, 1, 2, 3, 6):
+            gather(col)
+
+        def last_copies():
+            copies = []
+            for k, (a, b) in enumerate(((1, 0), (0, 1), (1, 1))):
+                span = {0: (1, 2), 1: (0, 1)}
+                land = {0: (0, 2), 1: (0, 1)}
+                copies.append(
+                    pltpu.make_async_remote_copy(
+                        src_ref=part.at[spans(span, a, b)],
+                        dst_ref=last_in.at[(k, *spans(land, a, b))],
+                        send_sem=part_send.at[k],
+                        recv_sem=part_recv.at[k],
+                        device_id=(wrap(mx - a), wrap(my - b)),
+                        device_id_type=MESH,
+                    )
                 )
-            )
-        for copy in copies:
-            copy.start()
-        for copy in copies:
-            copy.wait()
-        for cx in range(2):
-            for cy in range(2):
-                total = far[cx + 1, cy + 1]
-                if cx == 1:
-                    total = total + far_in[it, 0, 0, cy]
-                if cy == 1:
-                    total = total + far_in[it, 1, cx, 0]
-                if cx == 1 and cy == 1:
-                    total = total + far_in[it, 2, 0, 0]
-                field = (
-                    near[2 * cx + cy] - total + SELF_GAIN * moving[it, cx + 1, cy + 1]
-                )
-                tile = own[cx, cy]
-                result = tile[3:4] * (tile + field)
-                moving[it + 1, cx + 1, cy + 1] = result
-                for c in range(3):
-                    out[c, cx, cy : cy + 1] = result[c : c + 1]
+            return copies
+
+        @pl.when(it == ITERS - 1)
+        def _():
+            for copy in last_copies():
+                copy.start()
+
+        for col in (4, 5, 7, 8):
+            gather(col)
 
         @pl.when(it == 0)
         def _():
-            copies = halo(moving.at[1], 1)
+            copies = part_copies()
             for copy in copies:
                 copy.start()
             for copy in copies:
                 copy.wait()
+            reach = {0: ((-1, 0), (0, 0)), 1: ((0, 1),), 2: ((0, 2), (1, 0)), 3: ((1, 1),)}
+            for ex in range(4):
+                for ey in range(4):
+                    total = jnp.zeros((8, 128), F32)
+                    for a, i in reach[ex]:
+                        for b, j in reach[ey]:
+                            if a == 0 and b == 0:
+                                total = total + part[i, j]
+                            else:
+                                total = total + inbox[sides.index((a, b)), i, j]
+                    moving[1, ex, ey] = fixed[ex, ey, 7:8] * (fixed[ex, ey, 8:16] + total)
+
+        @pl.when(it == ITERS - 1)
+        def _():
+            for copy in last_copies():
+                copy.wait()
+            for cx in range(2):
+                for cy in range(2):
+                    total = part[cx + 1, cy + 1]
+                    if cx == 1:
+                        total = total + last_in[0, 0, cy]
+                    if cy == 1:
+                        total = total + last_in[1, cx, 0]
+                    if cx == 1 and cy == 1:
+                        total = total + last_in[2, 0, 0]
+                    tile = fixed[cx + 1, cy + 1]
+                    result = tile[7:8] * (tile[8:16] + total)
+                    for c in range(3):
+                        out[c, cx, cy : cy + 1] = result[c : c + 1]
 
         return carry
 
@@ -578,15 +632,18 @@
     return pl.pallas_call(
         kernel,
         out_shape=jax.ShapeDtypeStruct((3, 2, 2, 128), F32),
-        in_specs=[vmem] * (5 + len(TABLES)),
+        in_specs=[vmem] * 5 + [pl.BlockSpec(memory_space=pl.ANY)] * 2,
         out_specs=vmem,
         scratch_shapes=[
-            room(4, 4, 8, 128),
-            room(3, 4, 4, 8, 128),
-            room(2, 2, 8, 128),
+            room(2, 3 * N, N, dtype=BF16),
+            room(4, HALF, N),
+            room(4, 4, 16, 128),
+            room(2, 4, 4, 8, 128),
             room(9, 3, N, 128),
-            room(9, N, N, dtype=BF16),
-            room(9, N, N, dtype=BF16),
+            room(N, 9 * N, dtype=BF16),
+            room(N, 9 * N, dtype=BF16),
+            room(9 * N, N, dtype=BF16),
+            room(9 * N, N, dtype=BF16),
             room(N, 9 * N, dtype=BF16),
             room(N, 9 * N, dtype=BF16),
             room(N, N),
@@ -599,13 +656,15 @@
             room(36, 3, 6, 8, 128),
             room(4, 8, 128),
             room(3, 3, 8, 128),
-            room(2, 3, 2, 2, 8, 128),
+            room(8, 3, 3, 8, 128),
+            room(3, 2, 2, 8, 128),
+            dma((2,)),
             dma((4,)),
             dma((4,)),
-            dma((3, 8)),
-            dma((3, 8)),
-            dma((2, 3)),
-            dma((2, 3)),
+            dma((2, 8)),
+            dma((2, 8)),
+            dma((3,)),
+            dma((3,)),
             pltpu.SemaphoreType.REGULAR,
         ],
         compiler_params=pltpu.CompilerParams(

time: 95.2 us -> 84 us (0.88)
  Pallas kernels: 93.8 us -> 82.5 us
    pallas_call x1, Pallas kernels: 93.8 us -> 82.5 us  [shards(): pl.pallas_call(kernel, out_shape=jax.ShapeDtypeStruct((3, 2, 2, 128), F32...]
where the time goes in v1:
time: 84 us; the launch traced here: 83.8 us
  Pallas kernels  82.5 us (98%)
  local copies, waits for them, and re-layouts  1.29 us (2%)
    pallas_call x1, Pallas kernels, shards(): pl.pallas_call(kernel, out_shape=jax.ShapeDtypeStruct((3, 2, 2, 128), F32...  82.5 us

profile of v1, /device:TPU:1, one launch (start us, length us, event | category | flops | bytes accessed | tf_op | source)
XLA Modules:
  0.0 83.8 jit_solution(6570529593377626990)
XLA Ops:
  0.0 82.5 %shard_map.73 = f32[3,2,2,128]{3,2,1,0:T(2,128)} custom-call(f32[3,2,2,128]{3,2,1,0:T(2,128)} %cot.1, f32[2,2,128]{2,1,0:T(2,128)} %pol.1, s32[3,2,2,128]{3,2,1,0:T(2,128)} %off.1, f32[3,2,2,128]{3,2,1,0:T(2,128)} %frac.1, s32[2,2,16]{2,1,0:T(2,128)} %cnt.1, bf16[2,768,256]{2,1,0:T(8,128)(2,1)} %constant.4.clone.waves_far, ...), custom_call_target="tpu_custom_call" | custom-call | tf_op jit(solution)/shard_map/pallas_call | solution.py:632
  82.5 1.3 %copy.9 = f32[3,2,2,128]{3,2,1,0:T(2,128)} copy(f32[3,2,2,128]{3,2,1,0:T(2,128)} %shard_map.73) | data formatting | bytes 12288

commit v2 on v1

--- a/solution.py
+++ b/solution.py
@@ -95,6 +95,23 @@
 
 TABLES = tables()
 
+SUPPORT = {0: (0, 3), 1: (0, 11), 2: (8, 16)}
+
+
+def ring(offset, count):
+    return min(offset, count - offset)
+
+
+ROUTES = [
+    (dy, dx, dz, dc)
+    for dz in range(8)
+    for dy in range(4)
+    for dx in range(4)
+    for dc in range(2)
+    if (dy, dx, dz, dc) != (0, 0, 0, 0)
+]
+ROUTES.sort(key=lambda r: -(ring(r[0], 4) + ring(r[1], 4) + ring(r[2], 8)))
+
 NN = (((1,), (0,)), ((), ()))
 NT = (((1,), (1,)), ((), ()))
 
@@ -175,9 +192,9 @@
 
 
 def kernel(
-    cot, pol, off, frac, cnt, waves_far, plane_far,
+    cot_far, pol_far, off_far, frac_far, cnt_far, waves_far, plane_far,
     out,
-    waves, plane, fixed, moving, prod, wz_hi, wz_lo, wt_hi, wt_lo, p_hi, p_lo, spread,
+    cot, pol, off, frac, cnt, waves, plane, fixed, moving, prod, wz_hi, wz_lo, wt_hi, wt_lo, p_hi, p_lo, spread,
     send_a, send_b, land_a, land_b, near_static, near_moving, tensor, near, part, inbox, last_in,
     table_sem, send_s, recv_s, halo_send, halo_recv, part_send, part_recv, second_level,
 ):
@@ -188,6 +205,19 @@
     def wrap(i):
         return lax.rem(i + SIDE, SIDE)
 
+    arguments = [
+        pltpu.make_async_copy(source, target, table_sem.at[2 + k])
+        for k, (source, target) in enumerate(
+            ((cot_far, cot), (pol_far, pol), (off_far, off), (frac_far, frac), (cnt_far, cnt))
+        )
+    ]
+    table_copies = [
+        pltpu.make_async_copy(waves_far, waves, table_sem.at[0]),
+        pltpu.make_async_copy(plane_far, plane, table_sem.at[1]),
+    ]
+    for copy in arguments + table_copies:
+        copy.start()
+
     entry = pltpu.get_barrier_semaphore()
 
     def greet(i, carry):
@@ -202,13 +232,8 @@
                 entry, inc=1, device_id=(wrap(mx + a), wrap(my + b)), device_id_type=MESH
             )
 
-    table_copies = [
-        pltpu.make_async_copy(waves_far, waves, table_sem.at[0]),
-        pltpu.make_async_copy(plane_far, plane, table_sem.at[1]),
-    ]
-    for copy in table_copies:
-        copy.start()
-
+    for copy in arguments:
+        copy.wait()
     lane = lax.broadcasted_iota(jnp.int32, (8, 128), 1)
     row = lax.broadcasted_iota(jnp.int32, (8, 128), 0)
     expand = (
@@ -310,9 +335,8 @@
     low = lax.broadcasted_iota(jnp.int32, (SIDE, 128), 0)
     cell_z = lax.broadcasted_iota(jnp.int32, (1, 128), 1) // 8 * 16
 
-    def weights(col):
-        ex = col // 3
-        ey = lax.rem(col, 3)
+    def weights(ex, ey):
+        col = ex * 3 + ey
         tile = fixed[ex, ey]
         anchor = tile[0:3].astype(jnp.int32)
         value, slope = zip(*[spline(tile[c + 3 : c + 4]) for c in range(3)])
@@ -321,7 +345,7 @@
         place_z = (tall - (anchor[2:3] + cell_z)) & (N - 1)
         wx, sx = placed(place_x, value[0]), placed(place_x, slope[0])
         wy, sy = placed(place_y, value[1]), placed(place_y, slope[1])
-        for x in range(SIDE):
+        for x in range(*SUPPORT[ex]):
             rows = pl.ds(x * SIDE, SIDE)
             prod[col, 0, rows] = sx[x : x + 1] * wy
             prod[col, 1, rows] = wx[x : x + 1] * sy
@@ -332,18 +356,20 @@
             wz_hi[:, lanes], wz_lo[:, lanes] = halves(full)
             wt_hi[lanes, :], wt_lo[lanes, :] = halves(full.T)
 
-    def weights_own(i, carry):
-        weights((1 + i // 2) * 3 + 1 + lax.rem(i, 2))
-        return carry
-
-    def weights_other(i, carry):
-        weights(i + 2 * (i // 4))
-        return carry
-
-    lax.fori_loop(0, 4, weights_own, 0)
+    def weights_of(ex):
+        def body(ey, carry):
+            weights(ex, ey)
+            return carry
+
+        return body
+
+    lax.fori_loop(1, 3, weights_of(1), 0)
+    lax.fori_loop(1, 3, weights_of(2), 0)
     for copy in first_halo:
         copy.wait()
-    lax.fori_loop(0, 5, weights_other, 0)
+    lax.fori_loop(0, 3, weights_of(0), 0)
+    weights(1, 0)
+    weights(2, 0)
 
     def first_moment(col, carry):
         tile = fixed[col // 4, lax.rem(col, 4)]
@@ -416,21 +442,22 @@
         lax.fori_loop(0, 4, body, 0)
 
     def exchange(source, target, k):
-        def copy(t):
-            return pltpu.make_async_remote_copy(
-                src_ref=source.at[t],
+        for dy, dx, dz, dc in ROUTES:
+            to_y = lax.rem(mx // 4 + dy, 4)
+            to_x = lax.rem(my // 8 * 2 + lax.rem(mx // 2, 2) + dx, 4)
+            to_z = lax.rem(my + dz, 8)
+            to_core = lax.rem(mx + dc, 2)
+            gx = to_y * 4 + lax.rem(to_x, 2) * 2 + to_core
+            gy = to_x // 2 * 8 + to_z
+            pltpu.make_async_remote_copy(
+                src_ref=source.at[gx * SIDE + gy],
                 dst_ref=target.at[me],
                 send_sem=send_s.at[k],
                 recv_sem=recv_s.at[k],
-                device_id=(t // SIDE, lax.rem(t, SIDE)),
+                device_id=(gx, gy),
                 device_id_type=MESH,
-            )
-
-        def send(i, carry):
-            copy(lax.rem(me + i, N)).start()
-            return carry
-
-        lax.fori_loop(1, N, send, 0)
+            ).start()
+
         target[me] = source[me]
 
     def arrive(source, target, k):
@@ -491,21 +518,24 @@
         return product(cosine, first) + product(sine, other)
 
     def iteration(it, carry):
-        for group in range(3):
-            for col in range(3 * group, 3 * group + 3):
-                tile = moving[it, col // 3, col % 3]
-                plain = tile[0:1] * prod[col, 0] + tile[1:2] * prod[col, 1]
-                steep = tile[2:3] * prod[col, 2]
+        for ex in (1, 2, 0):
+            rows = slice(SUPPORT[ex][0] * SIDE, SUPPORT[ex][1] * SIDE)
+            for ey in range(3):
+                col = 3 * ex + ey
+                tile = moving[it, ex, ey]
+                plain = tile[0:1] * prod[col, 0, rows] + tile[1:2] * prod[col, 1, rows]
+                steep = tile[2:3] * prod[col, 2, rows]
                 left = slice(col * N, col * N + 128)
                 right = slice(col * N + 128, col * N + N)
-                p_hi[:, left], p_lo[:, left] = halves(plain)
-                p_hi[:, right], p_lo[:, right] = halves(steep)
-            span = slice(3 * N * group, 3 * N * (group + 1))
-            term = product((p_hi[:, span], p_lo[:, span]), (wt_hi[span], wt_lo[span]))
-            if group == 0:
-                spread[...] = term
+                p_hi[rows, left], p_lo[rows, left] = halves(plain)
+                p_hi[rows, right], p_lo[rows, right] = halves(steep)
+            span = slice(3 * N * ex, 3 * N * (ex + 1))
+            term = product((p_hi[rows, span], p_lo[rows, span]), (wt_hi[span], wt_lo[span]))
+            if ex == 1:
+                spread[rows] = term
+                spread[rows.stop :] = jnp.zeros((N - rows.stop, N), F32)
             else:
-                spread[...] += term
+                spread[rows] += term
 
         @pl.when(it == 0)
         def _():
@@ -535,15 +565,18 @@
 
         def gather(col):
             lanes = slice(col * N, col * N + N)
-            sampled = product(turned, (wz_hi[:, lanes], wz_lo[:, lanes]))
+            ex, ey = col // 3, col % 3
+            rows = slice(SUPPORT[ex][0] * SIDE, SUPPORT[ex][1] * SIDE)
+            sampled = product(
+                tuple(t[rows] for t in turned), (wz_hi[:, lanes], wz_lo[:, lanes])
+            )
             plain = sampled[:, :128]
             steep = sampled[:, 128:]
-            ex, ey = col // 3, col % 3
             total = jnp.concatenate(
                 [
-                    -jnp.sum(prod[col, 0] * plain, axis=0, keepdims=True),
-                    -jnp.sum(prod[col, 1] * plain, axis=0, keepdims=True),
-                    -jnp.sum(prod[col, 2] * steep, axis=0, keepdims=True),
+                    -jnp.sum(prod[col, 0, rows] * plain, axis=0, keepdims=True),
+                    -jnp.sum(prod[col, 1, rows] * plain, axis=0, keepdims=True),
+                    -jnp.sum(prod[col, 2, rows] * steep, axis=0, keepdims=True),
                     jnp.zeros((5, 128), F32),
                 ],
                 axis=0,
@@ -632,9 +665,14 @@
     return pl.pallas_call(
         kernel,
         out_shape=jax.ShapeDtypeStruct((3, 2, 2, 128), F32),
-        in_specs=[vmem] * 5 + [pl.BlockSpec(memory_space=pl.ANY)] * 2,
+        in_specs=[pl.BlockSpec(memory_space=pl.ANY)] * 7,
         out_specs=vmem,
         scratch_shapes=[
+            room(3, 2, 2, 128),
+            room(2, 2, 128),
+            room(3, 2, 2, 128, dtype=jnp.int32),
+            room(3, 2, 2, 128),
+            room(2, 2, 16, dtype=jnp.int32),
             room(2, 3 * N, N, dtype=BF16),
             room(4, HALF, N),
             room(4, 4, 16, 128),
@@ -658,7 +696,7 @@
             room(3, 3, 8, 128),
             room(8, 3, 3, 8, 128),
             room(3, 2, 2, 8, 128),
-            dma((2,)),
+            dma((7,)),
             dma((4,)),
             dma((4,)),
             dma((2, 8)),

time: 84 us -> 74.2 us (0.88)
  Pallas kernels: 82.5 us -> 72.7 us
    pallas_call x1, Pallas kernels: 82.5 us -> 72.7 us  [shards(): pl.pallas_call(kernel, out_shape=jax.ShapeDtypeStruct((3, 2, 2, 128), F32...]
where the time goes in v2:
time: 74.2 us; the launch traced here: 74 us
  Pallas kernels  72.7 us (98%)
  local copies, waits for them, and re-layouts  1.29 us (2%)
    pallas_call x1, Pallas kernels, shards(): pl.pallas_call(kernel, out_shape=jax.ShapeDtypeStruct((3, 2, 2, 128), F32...  72.7 us

profile of v2, /device:TPU:1, one launch (start us, length us, event | category | flops | bytes accessed | tf_op | source)
XLA Modules:
  0.0 74.0 jit_solution(6767507653171346178)
XLA Ops:
  0.0 72.7 %shard_map.73 = f32[3,2,2,128]{3,2,1,0:T(2,128)} custom-call(f32[3,2,2,128]{3,2,1,0:T(2,128)} %cot_far.1, f32[2,2,128]{2,1,0:T(2,128)} %pol_far.1, s32[3,2,2,128]{3,2,1,0:T(2,128)} %off_far.1, f32[3,2,2,128]{3,2,1,0:T(2,128)} %frac_far.1, s32[2,2,16]{2,1,0:T(2,128)} %cnt_far.1, bf16[2,768,256]{2,1,0:T(8,128)(2,1)} %constant.4.clone.waves_far, ...), custom_call_target="tpu_custom_call" | custom-call | tf_op jit(solution)/shard_map/pallas_call | solution.py:665
  72.7 1.3 %copy.9 = f32[3,2,2,128]{3,2,1,0:T(2,128)} copy(f32[3,2,2,128]{3,2,1,0:T(2,128)} %shard_map.73) | data formatting | bytes 12288

commit v3 on v2

--- a/solution.py
+++ b/solution.py
@@ -110,7 +110,14 @@
     for dc in range(2)
     if (dy, dx, dz, dc) != (0, 0, 0, 0)
 ]
-ROUTES.sort(key=lambda r: -(ring(r[0], 4) + ring(r[1], 4) + ring(r[2], 8)))
+
+
+def order(route):
+    across = ring(route[0], 4) + ring(route[1], 4)
+    return -(across + ring(route[2], 8)), -across, route[0], route[1]
+
+
+ROUTES.sort(key=order)
 
 NN = (((1,), (0,)), ((), ()))
 NT = (((1,), (1,)), ((), ()))
@@ -220,18 +227,26 @@
 
     entry = pltpu.get_barrier_semaphore()
 
-    def greet(i, carry):
-        pl.semaphore_signal(entry, inc=1, device_id=(wrap(mx + i), my), device_id_type=MESH)
-        pl.semaphore_signal(entry, inc=1, device_id=(mx, wrap(my + i)), device_id_type=MESH)
-        return carry
-
-    lax.fori_loop(1, SIDE, greet, 0)
-    for a in (-1, 1):
-        for b in (-1, 1):
-            pl.semaphore_signal(
-                entry, inc=1, device_id=(wrap(mx + a), wrap(my + b)), device_id_type=MESH
-            )
-
+    row_y, row_x, row_z = mx // 4, my // 8 * 2 + lax.rem(mx // 2, 2), lax.rem(my, 8)
+
+    def place(dy, dx, dz, dc):
+        to_y = lax.rem(row_y + dy, 4)
+        to_x = lax.rem(row_x + dx, 4)
+        to_core = lax.rem(mx + dc, 2)
+        return (
+            to_y * 4 + lax.rem(to_x, 2) * 2 + to_core,
+            to_x // 2 * 8 + lax.rem(row_z + dz, 8),
+        )
+
+    sides = [(a, b) for a in (-1, 0, 1) for b in (-1, 0, 1) if (a, b) != (0, 0)]
+    plane_peers = [r for r in ROUTES if r[2] == 0]
+    line_peers = [r for r in ROUTES if r[:2] == (0, 0) and r[3] == 0]
+    for route in plane_peers + line_peers:
+        pl.semaphore_signal(entry, inc=1, device_id=place(*route), device_id_type=MESH)
+    for a, b in sides:
+        pl.semaphore_signal(
+            entry, inc=1, device_id=(wrap(mx + a), wrap(my + b)), device_id_type=MESH
+        )
     for copy in arguments:
         copy.wait()
     lane = lax.broadcasted_iota(jnp.int32, (8, 128), 1)
@@ -255,15 +270,7 @@
                 axis=0,
             )
 
-    pl.semaphore_wait(entry, 2 * (SIDE - 1) + 4)
-
-    def second(i, carry):
-        pl.semaphore_signal(
-            second_level, inc=1, device_id=(wrap(mx + i), my), device_id_type=MESH
-        )
-        return carry
-
-    sides = [(a, b) for a in (-1, 0, 1) for b in (-1, 0, 1) if (a, b) != (0, 0)]
+    pl.semaphore_wait(entry, len(plane_peers) + len(line_peers) + len(sides))
 
     def spans(table, a, b):
         return tuple(pl.ds(*table[side]) for side in (a, b))
@@ -282,7 +289,10 @@
         )
     for copy in first_halo:
         copy.start()
-    lax.fori_loop(1, SIDE, second, 0)
+    for route in line_peers:
+        pl.semaphore_signal(
+            second_level, inc=1, device_id=place(*route), device_id_type=MESH
+        )
 
     taken = {-1: (2, 1), 0: (0, 3), 1: (0, 2)}
     inner = {-1: (0, 1), 0: (0, 3), 1: (0, 2)}
@@ -363,20 +373,47 @@
 
         return body
 
+    def spread_columns(it, groups, fresh):
+        for ex, first, last in groups:
+            rows = slice(SUPPORT[ex][0] * SIDE, SUPPORT[ex][1] * SIDE)
+            for ey in range(first, last):
+                col = 3 * ex + ey
+                tile = moving[it, ex, ey]
+                plain = tile[0:1] * prod[col, 0, rows] + tile[1:2] * prod[col, 1, rows]
+                steep = tile[2:3] * prod[col, 2, rows]
+                left = slice(col * N, col * N + 128)
+                right = slice(col * N + 128, col * N + N)
+                p_hi[rows, left], p_lo[rows, left] = halves(plain)
+                p_hi[rows, right], p_lo[rows, right] = halves(steep)
+            span = slice(N * (3 * ex + first), N * (3 * ex + last))
+            term = product((p_hi[rows, span], p_lo[rows, span]), (wt_hi[span], wt_lo[span]))
+            if fresh and ex == 1:
+                spread[rows] = term
+                spread[rows.stop :] = jnp.zeros((N - rows.stop, N), F32)
+            else:
+                spread[rows] += term
+
+    def first_moment(ex, ey):
+        tile = fixed[ex, ey]
+        moving[0, ex, ey] = tile[7:8] * tile[8:16]
+
+    owned = [(ex, ey) for ex in (1, 2) for ey in (1, 2)]
+    for ex, ey in owned:
+        first_moment(ex, ey)
     lax.fori_loop(1, 3, weights_of(1), 0)
     lax.fori_loop(1, 3, weights_of(2), 0)
+    spread_columns(0, ((1, 1, 3), (2, 1, 3)), True)
     for copy in first_halo:
         copy.wait()
-    lax.fori_loop(0, 3, weights_of(0), 0)
+    for ex in range(4):
+        for ey in range(4):
+            if (ex, ey) not in owned:
+                first_moment(ex, ey)
+    for ey in range(3):
+        weights(0, ey)
     weights(1, 0)
     weights(2, 0)
-
-    def first_moment(col, carry):
-        tile = fixed[col // 4, lax.rem(col, 4)]
-        moving[0, col // 4, lax.rem(col, 4)] = tile[7:8] * tile[8:16]
-        return carry
-
-    lax.fori_loop(0, 16, first_moment, 0)
+    spread_columns(0, ((1, 0, 1), (2, 0, 1), (0, 0, 3)), False)
 
     def pairs(item, carry):
         q = item // 9
@@ -442,13 +479,8 @@
         lax.fori_loop(0, 4, body, 0)
 
     def exchange(source, target, k):
-        for dy, dx, dz, dc in ROUTES:
-            to_y = lax.rem(mx // 4 + dy, 4)
-            to_x = lax.rem(my // 8 * 2 + lax.rem(mx // 2, 2) + dx, 4)
-            to_z = lax.rem(my + dz, 8)
-            to_core = lax.rem(mx + dc, 2)
-            gx = to_y * 4 + lax.rem(to_x, 2) * 2 + to_core
-            gy = to_x // 2 * 8 + to_z
+        for route in ROUTES:
+            gx, gy = place(*route)
             pltpu.make_async_remote_copy(
                 src_ref=source.at[gx * SIDE + gy],
                 dst_ref=target.at[me],
@@ -518,24 +550,9 @@
         return product(cosine, first) + product(sine, other)
 
     def iteration(it, carry):
-        for ex in (1, 2, 0):
-            rows = slice(SUPPORT[ex][0] * SIDE, SUPPORT[ex][1] * SIDE)
-            for ey in range(3):
-                col = 3 * ex + ey
-                tile = moving[it, ex, ey]
-                plain = tile[0:1] * prod[col, 0, rows] + tile[1:2] * prod[col, 1, rows]
-                steep = tile[2:3] * prod[col, 2, rows]
-                left = slice(col * N, col * N + 128)
-                right = slice(col * N + 128, col * N + N)
-                p_hi[rows, left], p_lo[rows, left] = halves(plain)
-                p_hi[rows, right], p_lo[rows, right] = halves(steep)
-            span = slice(3 * N * ex, 3 * N * (ex + 1))
-            term = product((p_hi[rows, span], p_lo[rows, span]), (wt_hi[span], wt_lo[span]))
-            if ex == 1:
-                spread[rows] = term
-                spread[rows.stop :] = jnp.zeros((N - rows.stop, N), F32)
-            else:
-                spread[rows] += term
+        @pl.when(it > 0)
+        def _():
+            spread_columns(it, ((1, 0, 3), (2, 0, 3), (0, 0, 3)), True)
 
         @pl.when(it == 0)
         def _():
@@ -546,7 +563,7 @@
 
         @pl.when(it == 0)
         def _():
-            pl.semaphore_wait(second_level, SIDE - 1)
+            pl.semaphore_wait(second_level, len(line_peers))
 
         exchange(send_a, land_a.at[it], 2 * it)
 

time: 74.2 us -> 71.9 us (0.969)
  Pallas kernels: 72.7 us -> 70.5 us
    pallas_call x1, Pallas kernels: 72.7 us -> 70.5 us  [shards(): pl.pallas_call(kernel, out_shape=jax.ShapeDtypeStruct((3, 2, 2, 128), F32...]
where the time goes in v3:
time: 71.9 us; the launch traced here: 71.8 us
  Pallas kernels  70.5 us (98%)
  local copies, waits for them, and re-layouts  1.29 us (2%)
    pallas_call x1, Pallas kernels, shards(): pl.pallas_call(kernel, out_shape=jax.ShapeDtypeStruct((3, 2, 2, 128), F32...  70.5 us

profile of v3, /device:TPU:1, one launch (start us, length us, event | category | flops | bytes accessed | tf_op | source)
XLA Modules:
  0.0 71.8 jit_solution(15067107362001260806)
XLA Ops:
  0.0 70.5 %shard_map.73 = f32[3,2,2,128]{3,2,1,0:T(2,128)} custom-call(f32[3,2,2,128]{3,2,1,0:T(2,128)} %cot_far.1, f32[2,2,128]{2,1,0:T(2,128)} %pol_far.1, s32[3,2,2,128]{3,2,1,0:T(2,128)} %off_far.1, f32[3,2,2,128]{3,2,1,0:T(2,128)} %frac_far.1, s32[2,2,16]{2,1,0:T(2,128)} %cnt_far.1, bf16[2,768,256]{2,1,0:T(8,128)(2,1)} %constant.4.clone.waves_far, ...), custom_call_target="tpu_custom_call" | custom-call | tf_op jit(solution)/shard_map/pallas_call | solution.py:682
  70.5 1.3 %copy.9 = f32[3,2,2,128]{3,2,1,0:T(2,128)} copy(f32[3,2,2,128]{3,2,1,0:T(2,128)} %shard_map.73) | data formatting | bytes 12288

commit v4 on v3

--- a/solution.py
+++ b/solution.py
@@ -341,9 +341,8 @@
 
         lax.fori_loop(0, 16, body, 0)
 
-    tall = lax.broadcasted_iota(jnp.int32, (N, 128), 0)
     low = lax.broadcasted_iota(jnp.int32, (SIDE, 128), 0)
-    cell_z = lax.broadcasted_iota(jnp.int32, (1, 128), 1) // 8 * 16
+    cell_z = lax.broadcasted_iota(jnp.int32, (SIDE, 128), 1) // 8
 
     def weights(ex, ey):
         col = ex * 3 + ey
@@ -352,7 +351,7 @@
         value, slope = zip(*[spline(tile[c + 3 : c + 4]) for c in range(3)])
         place_x = low - (anchor[0:1] + (ex - 1) * 8)
         place_y = low - (anchor[1:2] + (ey - 1) * 8)
-        place_z = (tall - (anchor[2:3] + cell_z)) & (N - 1)
+        place_z = low - anchor[2:3]
         wx, sx = placed(place_x, value[0]), placed(place_x, slope[0])
         wy, sy = placed(place_y, value[1]), placed(place_y, slope[1])
         for x in range(*SUPPORT[ex]):
@@ -361,7 +360,19 @@
             prod[col, 1, rows] = wx[x : x + 1] * sy
             prod[col, 2, rows] = wx[x : x + 1] * wy
         for k, source in enumerate((value[2], slope[2])):
-            full = placed(place_z, source)
+            base = placed(place_z, source)
+            spill = placed(place_z + SIDE, source)
+            full = jnp.concatenate(
+                [
+                    jnp.where(
+                        cell_z == cell,
+                        base,
+                        jnp.where(cell_z == (cell + SIDE - 1) % SIDE, spill, 0.0),
+                    )
+                    for cell in range(SIDE)
+                ],
+                axis=0,
+            )
             lanes = pl.ds(pl.multiple_of(col * N + 128 * k, 128), 128)
             wz_hi[:, lanes], wz_lo[:, lanes] = halves(full)
             wt_hi[lanes, :], wt_lo[lanes, :] = halves(full.T)
@@ -576,9 +587,20 @@
         put_rows(send_b, filtered(get_rows(land_a.at[it])))
         exchange(send_b, land_b.at[it], 2 * it + 1)
         near_field(it)
+
+        @pl.when(it == 0)
+        def _():
+            def fold(col, carry):
+                lanes = pl.ds(pl.multiple_of(col * N, N), N)
+                wz_hi[:, lanes], wz_lo[:, lanes] = halves(
+                    product(wave(0), (wz_hi[:, lanes], wz_lo[:, lanes]))
+                )
+                return carry
+
+            lax.fori_loop(0, 9, fold, 0)
+
         arrive(send_b, land_b.at[it], 2 * it + 1)
-        potential = product(wave(0), halves(get_rows(land_b.at[it])))
-        turned = halves(potential.T)
+        turned = halves(get_rows(land_b.at[it]).T)
 
         def gather(col):
             lanes = slice(col * N, col * N + N)

time: 71.9 us -> 70.7 us (0.983)
  Pallas kernels: 70.5 us -> 69.2 us
    pallas_call x1, Pallas kernels: 70.5 us -> 69.2 us  [shards(): pl.pallas_call(kernel, out_shape=jax.ShapeDtypeStruct((3, 2, 2, 128), F32...]
where the time goes in v4:
time: 70.7 us; the launch traced here: 70.5 us
  Pallas kernels  69.2 us (98%)
  local copies, waits for them, and re-layouts  1.29 us (2%)
    pallas_call x1, Pallas kernels, shards(): pl.pallas_call(kernel, out_shape=jax.ShapeDtypeStruct((3, 2, 2, 128), F32...  69.2 us

profile of v4, /device:TPU:1, one launch (start us, length us, event | category | flops | bytes accessed | tf_op | source)
XLA Modules:
  0.0 70.5 jit_solution(5433107449130530964)
XLA Ops:
  0.0 69.2 %shard_map.73 = f32[3,2,2,128]{3,2,1,0:T(2,128)} custom-call(f32[3,2,2,128]{3,2,1,0:T(2,128)} %cot_far.1, f32[2,2,128]{2,1,0:T(2,128)} %pol_far.1, s32[3,2,2,128]{3,2,1,0:T(2,128)} %off_far.1, f32[3,2,2,128]{3,2,1,0:T(2,128)} %frac_far.1, s32[2,2,16]{2,1,0:T(2,128)} %cnt_far.1, bf16[2,768,256]{2,1,0:T(8,128)(2,1)} %constant.4.clone.waves_far, ...), custom_call_target="tpu_custom_call" | custom-call | tf_op jit(solution)/shard_map/pallas_call | solution.py:704
  69.2 1.3 %copy.9 = f32[3,2,2,128]{3,2,1,0:T(2,128)} copy(f32[3,2,2,128]{3,2,1,0:T(2,128)} %shard_map.73) | data formatting | bytes 12288

commit v5 on v4

--- a/solution.py
+++ b/solution.py
@@ -523,6 +523,20 @@
     def get_rows(ref):
         return jnp.concatenate([ref[:, 0, :], ref[:, 1, :]], axis=1)
 
+    def fill_green():
+        line = jnp.zeros((1, 128), F32) + me.astype(F32)
+        signed = jnp.where(line < N // 2, line, line - N) * (1.0 / N)
+        height = signed * signed
+        bend = 2.0 + jnp.cos(line * (2.0 * math.pi / N))
+        strength = jnp.exp(-((math.pi / BETA) ** 2) * height) * 9.0 / (bend * bend)
+        height = jnp.concatenate([height, height], axis=1)
+        strength = jnp.concatenate([strength, strength], axis=1)
+        square = plane[3] + height
+        centre = square == 0.0
+        plane[2] = jnp.where(
+            centre, 0.0, plane[2] * strength / jnp.where(centre, 1.0, square)
+        )
+
     def filtered(value):
         cosine = wave(1)
         sine = wave(2)
@@ -537,18 +551,7 @@
         by_sine = product(both, sine)
         re = by_cosine[:HALF] - by_sine[HALF:]
         im = by_sine[:HALF] + by_cosine[HALF:]
-        line = jnp.zeros((1, 128), F32) + me.astype(F32)
-        signed = jnp.where(line < N // 2, line, line - N) * (1.0 / N)
-        height = signed * signed
-        bend = 2.0 + jnp.cos(line * (2.0 * math.pi / N))
-        strength = jnp.exp(-((math.pi / BETA) ** 2) * height) * 9.0 / (bend * bend)
-        height = jnp.concatenate([height, height], axis=1)
-        strength = jnp.concatenate([strength, strength], axis=1)
-        square = plane[3] + height
-        centre = square == 0.0
-        green = jnp.where(
-            centre, 0.0, plane[2] * strength / jnp.where(centre, 1.0, square)
-        )
+        green = plane[2]
         both = halves(jnp.concatenate([re * green, im * green], axis=0))
         by_cosine = product(both, cosine)
         by_sine = product(both, sine)
@@ -582,6 +585,7 @@
         def _():
             lax.fori_loop(0, 16, grow_static, 0)
             lax.fori_loop(0, 36, pairs, 0)
+            fill_green()
 
         arrive(send_a, land_a.at[it], 2 * it)
         put_rows(send_b, filtered(get_rows(land_a.at[it])))

time: 70.7 us -> 70.5 us (level)
  no operation moved by 1% of the time
where the time goes in v5:
time: 70.5 us; the launch traced here: 70.3 us
  Pallas kernels  69.1 us (98%)
  local copies, waits for them, and re-layouts  1.29 us (2%)
    pallas_call x1, Pallas kernels, shards(): pl.pallas_call(kernel, out_shape=jax.ShapeDtypeStruct((3, 2, 2, 128), F32...  69.1 us

profile of v5, /device:TPU:1, one launch (start us, length us, event | category | flops | bytes accessed | tf_op | source)
XLA Modules:
  0.0 70.3 jit_solution(3815799902439647347)
XLA Ops:
  0.0 69.1 %shard_map.73 = f32[3,2,2,128]{3,2,1,0:T(2,128)} custom-call(f32[3,2,2,128]{3,2,1,0:T(2,128)} %cot_far.1, f32[2,2,128]{2,1,0:T(2,128)} %pol_far.1, s32[3,2,2,128]{3,2,1,0:T(2,128)} %off_far.1, f32[3,2,2,128]{3,2,1,0:T(2,128)} %frac_far.1, s32[2,2,16]{2,1,0:T(2,128)} %cnt_far.1, bf16[2,768,256]{2,1,0:T(8,128)(2,1)} %constant.4.clone.waves_far, ...), custom_call_target="tpu_custom_call" | custom-call | tf_op jit(solution)/shard_map/pallas_call | solution.py:708
  69.1 1.3 %copy.9 = f32[3,2,2,128]{3,2,1,0:T(2,128)} copy(f32[3,2,2,128]{3,2,1,0:T(2,128)} %shard_map.73) | data formatting | bytes 12288
